TPU v7x, 32 devices: a 4x4x1 block of a 4x4x8 slice. The times are simulated.
32 devices in a mesh: rep: 1 (over z), tp: 4 (over y), sp: 8 (over x, core).
Axes of the slice: x: 4, y: 4, z: 1, core: 2. Of those that a mesh axis runs over, the one named last changes fastest.
The devices are a block of a 4x4x8 slice.
Arguments:
- x_in: bfloat16 [4096, 5120], P(('rep', 'sp'))
- positions: int32 [4096], P(('rep', 'sp'))
- norm_gain: float32 [5120], replicated
- w_q: bfloat16 [5120, 4096], P(None, 'tp')
- w_k: bfloat16 [5120, 1024], P(None, 'tp')
- w_v: bfloat16 [5120, 1024], P(None, 'tp')
- w_o: bfloat16 [4096, 5120], P('tp')
- w_gate: bfloat16 [5120, 32768], P(None, 'tp')
- w_up: bfloat16 [5120, 32768], P(None, 'tp')
- w_down: bfloat16 [32768, 5120], P('tp')
Outputs:
- output 1: bfloat16 [4096, 5120], P(('rep', 'sp'))
- output 2: bfloat16 [4096, 32, 128], P('rep', ('tp', 'sp'))
- output 3: bfloat16 [4096, 32, 128], P('rep', ('tp', 'sp'))
All inputs are finite; a program needn't handle non-finite values.
Results may differ from a plain program's by a relative error of at most 0.00236406.
Values are sent between devices in bfloat16 or wider.
A program may use at most 768 MiB of HBM per device.

v0:
```python
import jax
import jax.numpy as jnp
from jax import lax
from jax.sharding import PartitionSpec as P

HEAD_DIM = 128
EPS = 1e-6
ROPE_BASE = 500000.0
SCORE_SCALE = HEAD_DIM ** -0.5


def rms_norm(x_in, norm_gain):
    x_f32 = x_in.astype(jnp.float32)
    inv_rms = lax.rsqrt(jnp.mean(x_f32 * x_f32, axis=-1, keepdims=True) + EPS)
    return (x_f32 * inv_rms * norm_gain).astype(jnp.bfloat16)


def rope_tables(positions):
    inv_freq = ROPE_BASE ** (-(jnp.arange(HEAD_DIM // 2, dtype=jnp.float32) * (2.0 / HEAD_DIM)))
    angles = positions.astype(jnp.float32)[:, None] * inv_freq[None, :]
    return jnp.cos(angles)[:, None, :], jnp.sin(angles)[:, None, :]


def rotate(vectors, cos_tab, sin_tab):
    half_dim = HEAD_DIM // 2
    lower_part = vectors[..., :half_dim]
    upper_part = vectors[..., half_dim:]
    return jnp.concatenate([lower_part * cos_tab - upper_part * sin_tab, upper_part * cos_tab + lower_part * sin_tab], axis=-1).astype(jnp.bfloat16)


def gated_mlp(normed, w_gate, w_up, w_down):
    gate_acc = jnp.dot(normed, w_gate, preferred_element_type=jnp.float32)
    up_acc = jnp.dot(normed, w_up, preferred_element_type=jnp.float32)
    hidden = (jax.nn.silu(gate_acc) * up_acc).astype(jnp.bfloat16)
    return jnp.dot(hidden, w_down, preferred_element_type=jnp.float32)


def causal_attention(q_rows, k_keys, v_keys, q_offset):
    tokens_q = q_rows.shape[0]
    heads_here = q_rows.shape[1]
    key_count = k_keys.shape[0]
    cache_here = k_keys.shape[1]
    group_size = heads_here // cache_here
    tile_rows = min(tokens_q, 128)
    key_idx = jnp.arange(key_count)

    def attend_tile(tile_id):
        q_tile = lax.dynamic_slice_in_dim(q_rows, tile_id * tile_rows, tile_rows, axis=0).reshape(tile_rows, cache_here, group_size, HEAD_DIM)
        scores = jnp.einsum("qcgd,kcd->cgqk", q_tile, k_keys, preferred_element_type=jnp.float32) * SCORE_SCALE
        query_idx = q_offset + tile_id * tile_rows + jnp.arange(tile_rows)
        scores = jnp.where(key_idx[None, :] <= query_idx[:, None], scores, -jnp.inf)
        weights = jnp.exp(scores - jnp.max(scores, axis=-1, keepdims=True))
        weight_total = jnp.sum(weights, axis=-1)
        weighted_sum = jnp.einsum("cgqk,kcd->qcgd", weights.astype(jnp.bfloat16), v_keys, preferred_element_type=jnp.float32)
        return (weighted_sum / jnp.transpose(weight_total, (2, 0, 1))[..., None]).astype(jnp.bfloat16)

    attn_tiles = lax.map(attend_tile, jnp.arange(tokens_q // tile_rows))
    return attn_tiles.reshape(tokens_q, heads_here, HEAD_DIM)


def solution(mesh):
    sp_size = mesh.shape["sp"]
    row_spec = P(("rep", "sp"), None)
    cache_spec = P("rep", ("tp", "sp"), None)

    def layer_block(x_in, positions, norm_gain, w_q, w_k, w_v, w_o, w_gate, w_up, w_down):
        tok_local = x_in.shape[0]
        heads_tp = w_q.shape[1] // HEAD_DIM
        kv_tp = w_k.shape[1] // HEAD_DIM
        heads_dev = heads_tp // sp_size
        cache_tp = max(kv_tp, sp_size)
        cache_dev = cache_tp // sp_size
        kv_repeat = cache_tp // kv_tp
        normed = rms_norm(x_in, norm_gain)
        cos_tab, sin_tab = rope_tables(positions)
        q_rot = rotate(jnp.dot(normed, w_q, preferred_element_type=jnp.float32).reshape(tok_local, heads_tp, HEAD_DIM), cos_tab, sin_tab)
        k_rot = rotate(jnp.dot(normed, w_k, preferred_element_type=jnp.float32).reshape(tok_local, kv_tp, HEAD_DIM), cos_tab, sin_tab)
        v_val = jnp.dot(normed, w_v, preferred_element_type=jnp.float32).astype(jnp.bfloat16).reshape(tok_local, kv_tp, HEAD_DIM)
        q_send = q_rot.reshape(tok_local, sp_size, heads_dev, HEAD_DIM)
        k_send = jnp.repeat(k_rot, kv_repeat, axis=1).reshape(tok_local, sp_size, cache_dev, HEAD_DIM)
        v_send = jnp.repeat(v_val, kv_repeat, axis=1).reshape(tok_local, sp_size, cache_dev, HEAD_DIM)
        send_buf = jnp.concatenate([q_send, k_send, v_send], axis=2)
        recv_buf = lax.all_to_all(send_buf, "sp", 1, 0, tiled=True)
        recv_buf = recv_buf.reshape(tok_local * sp_size, heads_dev + 2 * cache_dev, HEAD_DIM)
        q_all = recv_buf[:, :heads_dev]
        k_all = recv_buf[:, heads_dev:heads_dev + cache_dev]
        v_all = recv_buf[:, heads_dev + cache_dev:]
        attn_heads = causal_attention(q_all, k_all, v_all, 0)
        attn_tok = lax.all_to_all(attn_heads, "sp", 0, 1, tiled=True).reshape(tok_local, heads_tp * HEAD_DIM)
        attn_sum = lax.psum(jnp.dot(attn_tok, w_o, preferred_element_type=jnp.float32), "tp")
        mlp_sum = lax.psum(gated_mlp(normed, w_gate, w_up, w_down), "tp")
        y_out = (x_in.astype(jnp.float32) + attn_sum + mlp_sum).astype(jnp.bfloat16)
        return y_out, k_all, v_all

    return jax.shard_map(
        layer_block,
        mesh=mesh,
        in_specs=(row_spec, P(("rep", "sp")), P(None), P(None, "tp"), P(None, "tp"), P(None, "tp"), P("tp", None), P(None, "tp"), P(None, "tp"), P("tp", None)),
        out_specs=(row_spec, cache_spec, cache_spec),
        check_vma=False,
    )
```

profile of v0, /device:TPU:97, one launch (start us, length us, event | category | flops | bytes accessed | tf_op | source)
XLA Modules:
  0.0 755.9 jit_solution(13312546295108773464)
XLA Ops:
  8.1 3.6 fusion.18
  12.5 5.1 convolution_convert_fusion
  18.7 5.2 fusion.33
  24.2 10.0 %convolution_bitcast_fusion.1 = f32[64,8,8,128]{3,1,2,0:T(8,128)S(1)} fusion(bf16[5120,1024]{1,0:T(8,128)(2,1)} %param.15, bf16[512,5120]{1,0:T(8,128)(2,1)} %param.12, f32[5120]{0:T(1024)S(1)} %copy-done.4, f32[512]{0:T(512)S(1)} %add_rsqrt_fusion), kind=kOutput, calls=%fused_computation.35 | convolution fusion | flops 5379194880 | bytes 17848320 | tf_op jit(solution)/shard_map/dot_general | solution.py:76
  36.4 2.0 pad_maximum_fusion
  38.4 6.4 all-to-all-start
  44.9 51.9 %fusion.30 = f32[512,8192]{1,0:T(8,128)} fusion(bf16[5120,8192]{1,0:T(8,128)(2,1)} %param.19, bf16[512,5120]{1,0:T(8,128)(2,1)} %param.12, f32[5120]{0:T(1024)S(1)} %copy-done.4, f32[512]{0:T(512)S(1)} %add_rsqrt_fusion), kind=kOutput, calls=%fused_computation.47 | convolution fusion | flops 42960158720 | bytes 105928704 | tf_op jit(solution)/shard_map/dot_general | solution.py:32
  96.8 58.3 %multiply_convert_fusion.clone.4 = bf16[512,8192]{1,0:T(8,128)(2,1)} fusion(f32[512,8192]{1,0:T(8,128)} %fusion.30, bf16[5120,8192]{1,0:T(8,128)(2,1)} %param.20, bf16[512,5120]{1,0:T(8,128)(2,1)} %param.12, f32[5120]{0:T(1024)S(1)} %copy-done.4, f32[512]{0:T(512)S(1)} %add_rsqrt_fusion), kind=kOutput, calls=%fused_computation.21.clone.clone.clone.1 | convolution fusion | flops 42985324544 | bytes 114317312 | tf_op jit(solution)/shard_map/dot_general | solution.py:33
  155.0 2.2 copy.57
  158.4 134.3 %while.11 = (s32[]{:T(128)}, bf16[32,128,1,1,128]{4,1,3,2,0:T(8,128)(2,1)}, s32[32]{0:T(128)S(1)}, bf16[4096,1,128]{2,0,1:T(8,128)(2,1)}, bf16[4096,1,128]{2,0,1...) while((s32[]{:T(128)}, ...), condition=%wide.region_4.5_spmd.clone, body=%wide.region_1.4_spmd.clone.sunk | while | flops 272662400 | bytes 8457907 | solution.py:57
  163.8 1.3 fusion.66
  210.0 1.3 fusion.66
  214.2 1.3 fusion.66
  226.8 1.3 fusion.66
  251.9 1.3 fusion.66
  293.3 3.3 reduce.2
  296.6 2.2 reshape.206
  298.7 5.1 all-to-all-start.1
  303.8 54.0 %fusion.23 = f32[512,5120]{1,0:T(8,128)} fusion(bf16[8192,5120]{1,0:T(8,128)(2,1)} %param.21, bf16[512,8192]{1,0:T(8,128)(2,1)} %multiply_convert_fusion.clone.4), kind=kOutput, calls=%fused_computation.30 | convolution fusion | flops 42949672960 | bytes 102760448 | tf_op jit(solution)/shard_map/dot_general | solution.py:35
  357.8 4.3 reshape.207
  363.2 1.5 copy.59
  364.7 12.2 %fusion.39 = f32[512,5120]{1,0:T(8,128)} fusion(bf16[512,1024]{0,1:T(8,128)(2,1)S(1)} %bitcast.99, bf16[1024,5120]{1,0:T(8,128)(2,1)} %param.18), kind=kOutput, calls=%fused_computation.52 | convolution fusion | flops 5368709120 | bytes 22020096 | tf_op jit(solution)/shard_map/dot_general | solution.py:90
  377.0 360.2 %all-reduce.3.cloned.1.call-done = (f32[512,5120]{1,0:T(8,128)}, f32[512,5120]{1,0:T(8,128)}) async-done(((f32[512,5120]{1,0:T(8,128)}, f32[512,5120]{1,0:T(8,128)}), (f32[512,5120]{1,0:T(8,128)}, f32[512,5120]{1,0:T(8,128)})) %all-reduce.3.cloned.1.call-update) | async-done | bytes 20971536 | tf_op jit(solution)/shard_map/psum | solution.py:91
  737.1 11.9 %fusion.22 = bf16[512,5120]{1,0:T(8,128)(2,1)} fusion(f32[512,5120]{1,0:T(8,128)} %get-tuple-element.73, f32[512,5120]{1,0:T(8,128)} %get-tuple-element.74, bf16[512,5120]{1,0:T(8,128)(2,1)} %param.12), kind=kLoop, calls=%fused_computation.29 | loop fusion | flops 10485760 | bytes 31457280 | tf_op jit(solution)/shard_map/convert_element_type | solution.py:92
  (189 shorter events, 114.5 us)
Async XLA Ops:
  7.2 5.3 copy-start
  7.2 5.3 copy-start.4
  38.4 116.6 %all-to-all-start = ((bf16[512,8,3,128]{3,0,2,1:T(8,128)(2,1)}), bf16[512,8,3,128]{3,0,2,1:T(8,128)(2,1)}, u32[]{:S(2)}, u32[]{:S(2)}) async-start(bf16[512,8,3,128]{3,0,2,1:T(8,128)(2,1)} %pad_maximum_fusion), calls=%async_computation | async-start | bytes 6291456 | tf_op jit(solution)/shard_map/all_to_all | solution.py:83
  292.7 65.1 %copy-start.2 = (bf16[4096,1,128]{2,0,1:T(8,128)(2,1)}, bf16[4096,1,128]{2,0,1:T(8,128)(2,1)S(1)}, u32[]{:S(2)}) copy-start(bf16[4096,1,128]{2,0,1:T(8,128)(2,1)S(1)} %get-tuple-element.165) | copy-start | bytes 3145732
  292.7 65.1 %copy-start.3 = (bf16[4096,1,128]{2,0,1:T(8,128)(2,1)}, bf16[4096,1,128]{2,0,1:T(8,128)(2,1)S(1)}, u32[]{:S(2)}) copy-start(bf16[4096,1,128]{2,0,1:T(8,128)(2,1)S(1)} %get-tuple-element.166) | copy-start | bytes 3145732
  298.7 59.1 %all-to-all-start.1 = ((bf16[8,2,32768]{2,1,0:T(2,128)(2,1)}), bf16[8,2,32768]{2,1,0:T(2,128)(2,1)}, u32[]{:S(2)}, u32[]{:S(2)}) async-start(bf16[8,2,32768]{2,1,0:T(2,128)(2,1)} %reshape.206), calls=%async_computation.1 | async-start | bytes 2097152 | tf_op jit(solution)/shard_map/all_to_all | solution.py:89
  303.8 433.3 %all-reduce.3.cloned.1.call-start = ((), (), s32[]{:S(2)}) async-start(), calls=%async_computation.2 | async-start | bytes 41943040 | tf_op jit(solution)/shard_map/psum | solution.py:91
  737.1 11.9 %copy-start.1 = (bf16[5120,256]{1,0:T(8,128)(2,1)S(1)}, bf16[5120,256]{1,0:T(8,128)(2,1)}, u32[]{:S(2)}) copy-start(bf16[5120,256]{1,0:T(8,128)(2,1)} %param.17) | copy-start | bytes 7864324
Sparse Core Ops, SparseCore 0:
  377.1 360.0 all-reduce.2
where the time goes:
time: 759 us; the launch traced here: 756 us
  waiting for transfers between devices  360 us (47%)
  matrix products  276 us (36%)
  other arithmetic  37.6 us (5%)
  local copies, waits for them, and re-layouts  34.6 us (5%)
  loops' own time  21.3 us (3%)
  between operations  14.2 us (2%)
  starting transfers between devices  11.5 us (2%)
    psum x1, waiting for transfers between devices, layer_block(): mlp_sum = lax.psum(gated_mlp(normed, w_gate, w_up, w_down), 'tp')  360 us
    dot_general x1, matrix products, gated_mlp(): up_acc = jnp.dot(normed, w_up, preferred_element_type=jnp.float32)  58.3 us
    dot_general x1, matrix products, gated_mlp(): return jnp.dot(hidden, w_down, preferred_element_type=jnp.float32)  54 us
    dot_general x1, matrix products, gated_mlp(): gate_acc = jnp.dot(normed, w_gate, preferred_element_type=jnp.float32)  51.9 us
    dot_general x32, matrix products, attend_tile(): jnp.einsum('qcgd,kcd->cgqk', q_tile, k_keys, preferred_element_type=jnp.f...  42.8 us
    dot_general x32, matrix products, attend_tile(): jnp.einsum('cgqk,kcd->qcgd', weights.astype(jnp.bfloat16), v_keys, prefer...  37.2 us
    another operation x1, loops' own time, causal_attention(): attn_tiles = lax.map(attend_tile, jnp.arange(tokens_q // tile_rows))  21.3 us
    dynamic_slice x32, local copies, waits for them, and re-layouts, causal_attention(): attn_tiles = lax.map(attend_tile, jnp.arange(tokens_q // tile_rows))  18.6 us
  transfers between devices with their start and end apart: 3, of which 1 were waited for; matrix products, arithmetic and copies ran while one was open for 22% of the time, Pallas kernels for 0%

commit v1 on v0

v1 whole, which is shorter than its diff:
```python
import functools

import jax
import jax.numpy as jnp
from jax import lax
from jax.experimental import pallas as pl
from jax.experimental.pallas import tpu as pltpu
from jax.sharding import PartitionSpec as P

HEAD_DIM = 128
EPS = 1e-6
ROPE_BASE = 500000.0
SCORE_SCALE = HEAD_DIM ** -0.5
F32 = jnp.float32
BF16 = jnp.bfloat16
MESH = pl.DeviceIdType.MESH
VMEM_LIMIT = 66 * 1000 * 1000

GW = 256
NW = 2 * GW
TW = 256
HW = TW // 2
SLOTS = 3
LAG = 2


def rms_norm(x_in, norm_gain):
    x_f32 = x_in.astype(F32)
    inv_rms = lax.rsqrt(jnp.mean(x_f32 * x_f32, axis=-1, keepdims=True) + EPS)
    return (x_f32 * inv_rms * norm_gain).astype(BF16)


def rope_tables(positions):
    inv_freq = ROPE_BASE ** (-(jnp.arange(HEAD_DIM // 2, dtype=F32) * (2.0 / HEAD_DIM)))
    angles = positions.astype(F32)[:, None] * inv_freq[None, :]
    return jnp.cos(angles)[:, None, :], jnp.sin(angles)[:, None, :]


def rotate(vectors, cos_tab, sin_tab):
    half_dim = HEAD_DIM // 2
    lower_part = vectors[..., :half_dim]
    upper_part = vectors[..., half_dim:]
    return jnp.concatenate([lower_part * cos_tab - upper_part * sin_tab, upper_part * cos_tab + lower_part * sin_tab], axis=-1).astype(BF16)


def attention_kernel(q_ref, k_ref, v_ref, o_ref, s_ref, *, rows):
    tile = pl.program_id(0)

    def score(block, masked):
        keys = k_ref[pl.ds(block * rows, rows), :]
        s = lax.dot_general(q_ref[...], keys, (((1,), (1,)), ((), ())), preferred_element_type=F32)
        if masked:
            row = lax.broadcasted_iota(jnp.int32, (rows, rows), 0)
            col = lax.broadcasted_iota(jnp.int32, (rows, rows), 1)
            s = jnp.where(col <= row, s, -jnp.inf)
        s_ref[block] = s
        top = s[:, :128]
        for g in range(1, rows // 128):
            top = jnp.maximum(top, s[:, g * 128:(g + 1) * 128])
        return top

    top = score(tile, True)
    top = lax.fori_loop(0, tile, lambda b, t: jnp.maximum(t, score(b, False)), top)
    row_max = jnp.max(top, axis=-1, keepdims=True) * SCORE_SCALE

    def gather(block, carry):
        total, acc = carry
        p = jnp.exp(s_ref[block] * SCORE_SCALE - row_max)
        for g in range(rows // 128):
            total = total + p[:, g * 128:(g + 1) * 128]
        acc = acc + jnp.dot(p.astype(BF16), v_ref[pl.ds(block * rows, rows), :], preferred_element_type=F32)
        return total, acc

    zero = jnp.zeros((rows, HEAD_DIM), F32)
    total, acc = lax.fori_loop(0, tile + 1, gather, (zero, zero))
    o_ref[...] = (acc / jnp.sum(total, axis=-1, keepdims=True)).astype(BF16)


def attention(q_all, k_all, v_all):
    tokens = q_all.shape[0]
    rows = min(512, tokens)
    tiles = tokens // rows
    whole = pl.BlockSpec((tokens, HEAD_DIM), lambda t: (0, 0))
    part = pl.BlockSpec((rows, HEAD_DIM), lambda t: (t, 0))
    return pl.pallas_call(
        functools.partial(attention_kernel, rows=rows),
        grid=(tiles,),
        out_shape=jax.ShapeDtypeStruct((tokens, HEAD_DIM), BF16),
        in_specs=[part, whole, whole],
        out_specs=part,
        scratch_shapes=[pltpu.VMEM((tiles, rows, rows), F32)],
        compiler_params=pltpu.CompilerParams(vmem_limit_bytes=48 * 1000 * 1000),
        cost_estimate=pl.CostEstimate(flops=2 * tokens * tokens * HEAD_DIM, bytes_accessed=8 * tokens * HEAD_DIM, transcendentals=tokens * tokens // 2),
    )(q_all, k_all, v_all)


def ring_kernel(
    ring,
    u_hbm, x_hbm, attn_hbm, wo_hbm, wg_hbm, wu_hbm, wd_hbm,
    y_hbm,
    slots, u, attn, xown, hid, part, far, near, ybuf,
    w_sem, ld_sem, far_sem, near_sem, ag_sem, fw_sem, send_sem, out_sem,
):
    tokens, width = u.shape
    ff = hid.shape[1]
    heads = attn.shape[1]
    rows = tokens // 2
    own = rows // ring
    gu_steps = ff // GW
    dn_tiles = width // NW
    chunk_steps = gu_steps + 2 * dn_tiles
    depth = (ff + heads) // 2
    tiles = width // TW
    all_tiles = 2 * tiles

    me = lax.axis_index("tp")
    right = lax.rem(me + 1, ring)
    left = lax.rem(me + ring - 1, ring)
    opp = lax.rem(me + 2, ring)

    def block_rows(owner):
        return pl.ds(pl.multiple_of(owner * own, own), own)

    def local(src, dst, sem):
        return pltpu.make_async_copy(src, dst, sem)

    def remote(src, dst, send, recv, who):
        return pltpu.make_async_remote_copy(src_ref=src, dst_ref=dst, send_sem=send, recv_sem=recv, device_id={"tp": who}, device_id_type=MESH)


    def issue(step):
        r = lax.rem(step, chunk_steps)
        slot = lax.rem(step, SLOTS)
        live = step < 2 * chunk_steps
        q = r - gu_steps
        tile_cols = pl.ds(pl.multiple_of(lax.div(jnp.maximum(q, 0), 2) * NW, NW), NW)

        @pl.when(jnp.logical_and(live, r < gu_steps))
        def _():
            cols = pl.ds(pl.multiple_of(r * GW, GW), GW)
            local(wg_hbm.at[:, cols], slots.at[slot, 0:width, 0:GW], w_sem.at[slot]).start()
            local(wu_hbm.at[:, cols], slots.at[slot, 0:width, GW:NW], w_sem.at[slot]).start()

        @pl.when(jnp.logical_and(live, jnp.logical_and(q >= 0, lax.rem(q, 2) == 0)))
        def _():
            local(wd_hbm.at[0:depth, tile_cols], slots.at[slot, 0:depth, :], w_sem.at[slot]).start()

        @pl.when(jnp.logical_and(live, jnp.logical_and(q >= 0, lax.rem(q, 2) == 1)))
        def _():
            local(wd_hbm.at[depth:ff, tile_cols], slots.at[slot, 0:ff - depth, :], w_sem.at[slot]).start()
            local(wo_hbm.at[:, tile_cols], slots.at[slot, ff - depth:depth, :], w_sem.at[slot]).start()

    def arrived(step, deep):
        slot = lax.rem(step, SLOTS)
        local(wd_hbm.at[0:deep, 0:NW], slots.at[slot, 0:deep, :], w_sem.at[slot]).wait()
        return slot


    def tick_pre(k):
        @pl.when(jnp.logical_and(k >= LAG, k < all_tiles + LAG))
        def _():
            t = k - LAG
            local(far.at[t], far.at[t], far_sem.at[t]).wait()
            part[t, block_rows(left), 0:HW] += far[t, 0]
            part[t, block_rows(right), HW:TW] += far[t, 1]

        @pl.when(jnp.logical_and(k >= 2 * LAG, k < all_tiles + 2 * LAG))
        def _():
            t = k - 2 * LAG
            local(near.at[t], near.at[t], near_sem.at[t]).wait()
            chunk = lax.div(t, tiles)
            cols = pl.ds(pl.multiple_of(lax.rem(t, tiles) * TW, TW), TW)
            total = (part[t, block_rows(me), :] + near[t, 0]) + near[t, 1]
            ybuf[t, block_rows(me), :] = (xown[chunk, :, cols].astype(F32) + total).astype(BF16)

    def tick_post(k):
        @pl.when(jnp.logical_and(k >= 3 * LAG, k < all_tiles + 3 * LAG))
        def _():
            t = k - 3 * LAG
            local(ybuf.at[t, 0:2 * own], ybuf.at[t, 0:2 * own], ag_sem.at[t]).wait()
            here = ybuf.at[t, block_rows(right), 0:HW]
            remote(here, here, send_sem.at[3], fw_sem.at[t], left).start()
            here = ybuf.at[t, block_rows(left), HW:TW]
            remote(here, here, send_sem.at[3], fw_sem.at[t], right).start()

        @pl.when(jnp.logical_and(k >= 2 * LAG, k < all_tiles + 2 * LAG))
        def _():
            t = k - 2 * LAG
            here = ybuf.at[t, block_rows(me), :]
            remote(here, here, send_sem.at[2], ag_sem.at[t], left).start()
            remote(here, here, send_sem.at[2], ag_sem.at[t], right).start()

        @pl.when(jnp.logical_and(k >= LAG, k < all_tiles + LAG))
        def _():
            t = k - LAG
            remote(part.at[t, block_rows(left), 0:HW], near.at[t, 0, :, 0:HW], send_sem.at[1], near_sem.at[t], left).start()
            remote(part.at[t, block_rows(right), HW:TW], near.at[t, 1, :, HW:TW], send_sem.at[1], near_sem.at[t], right).start()

        @pl.when(k < all_tiles)
        def _():
            t = k
            remote(part.at[t, block_rows(opp), 0:HW], far.at[t, 0], send_sem.at[0], far_sem.at[t], left).start()
            remote(part.at[t, block_rows(opp), HW:TW], far.at[t, 1], send_sem.at[0], far_sem.at[t], right).start()
            remote(part.at[t, block_rows(left), HW:TW], near.at[t, 0, :, HW:TW], send_sem.at[0], near_sem.at[t], left).start()
            remote(part.at[t, block_rows(right), 0:HW], near.at[t, 1, :, 0:HW], send_sem.at[0], near_sem.at[t], right).start()

        @pl.when(k >= 4 * LAG)
        def _():
            t = k - 4 * LAG
            local(ybuf.at[t, 0:own], ybuf.at[t, 0:own], fw_sem.at[t]).wait()
            there = y_hbm.at[pl.ds(pl.multiple_of(lax.div(t, tiles) * rows, rows), rows), pl.ds(pl.multiple_of(lax.rem(t, tiles) * TW, TW), TW)]
            local(ybuf.at[t], there, out_sem).start()


    for step in range(SLOTS - 1):
        issue(jnp.int32(step))
    loads = [local(u_hbm, u, ld_sem.at[0]), local(attn_hbm, attn, ld_sem.at[1])]
    for chunk in range(2):
        mine = pl.ds(pl.multiple_of(chunk * rows + me * own, own), own)
        loads.append(local(x_hbm.at[mine, :], xown.at[chunk], ld_sem.at[2 + chunk]))
    for load in loads:
        load.start()

    barrier = pltpu.get_barrier_semaphore()
    for neighbour in (left, right):
        pl.semaphore_signal(barrier, inc=1, device_id={"tp": neighbour}, device_id_type=MESH)
    pl.semaphore_wait(barrier, 2)
    for load in loads:
        load.wait()

    gu_ticks = tiles - dn_tiles
    period = gu_steps // gu_ticks

    def chunk_body(chunk, carry):
        base = chunk * chunk_steps
        row0 = pl.multiple_of(chunk * rows, rows)

        def gu_body(j, c):
            step = base + j
            ticks = jnp.logical_and(jnp.logical_and(chunk == 1, lax.rem(j, period) == period - 1), lax.div(j, period) < gu_ticks)
            k = dn_tiles - 1 + lax.div(j, period)

            @pl.when(ticks)
            def _():
                tick_pre(k)

            issue(step + SLOTS - 1)
            slot = arrived(step, width)
            both = jnp.dot(u[pl.ds(row0, rows), :], slots[slot, 0:width, :], preferred_element_type=F32)
            gate = both[:, :GW]
            act = (gate * jax.nn.sigmoid(gate)) * both[:, GW:]
            hid[:, pl.ds(pl.multiple_of(j * GW, GW), GW)] = act.astype(BF16)

            @pl.when(ticks)
            def _():
                tick_post(k)

            return c

        lax.fori_loop(0, gu_steps, gu_body, 0)

        def dn_body(j, c):
            step = base + gu_steps + 2 * j
            k = chunk * tiles + j - 1
            t = chunk * tiles + 2 * j

            @pl.when(k >= 0)
            def _():
                tick_pre(k)

            issue(step + SLOTS - 1)
            slot = arrived(step, depth)
            first = jnp.dot(hid[:, 0:depth], slots[slot, 0:depth, :], preferred_element_type=F32)
            for half in range(NW // TW):
                part[t + half] = first[:, half * TW:(half + 1) * TW]

            @pl.when(k >= 0)
            def _():
                tick_post(k)

            issue(step + SLOTS)
            slot = arrived(step + 1, depth)
            second = jnp.dot(hid[:, depth:ff], slots[slot, 0:ff - depth, :], preferred_element_type=F32)
            second = second + jnp.dot(attn[pl.ds(row0, rows), :], slots[slot, ff - depth:depth, :], preferred_element_type=F32)
            for half in range(NW // TW):
                part[t + half] += second[:, half * TW:(half + 1) * TW]
            return c

        lax.fori_loop(0, dn_tiles, dn_body, 0)
        return carry

    lax.fori_loop(0, 2, chunk_body, 0)

    def tail_body(k, c):
        tick_pre(k)
        tick_post(k)
        return c

    lax.fori_loop(tiles + dn_tiles - 1, all_tiles + 4 * LAG, tail_body, 0)

    local(part.at[0:tiles], part.at[0:tiles], send_sem.at[0]).wait()
    local(far, far, send_sem.at[1]).wait()
    local(ybuf.at[0:tiles], ybuf.at[0:tiles], send_sem.at[2]).wait()
    local(ybuf.at[0:tiles // 2], ybuf.at[0:tiles // 2], send_sem.at[3]).wait()
    local(ybuf, ybuf, out_sem).wait()


def ring_mlp(ring, normed, x_in, attn_tok, w_o, w_gate, w_up, w_down):
    tokens, width = x_in.shape
    ff = w_down.shape[0]
    heads = w_o.shape[0]
    rows = tokens // 2
    own = rows // ring
    all_tiles = 2 * (width // TW)
    depth = (ff + heads) // 2
    anywhere = pl.BlockSpec(memory_space=pl.ANY)
    flops = 2 * tokens * width * (3 * ff + heads)
    return pl.pallas_call(
        functools.partial(ring_kernel, ring),
        out_shape=jax.ShapeDtypeStruct((tokens, width), BF16),
        in_specs=[anywhere] * 7,
        out_specs=anywhere,
        scratch_shapes=[
            pltpu.VMEM((SLOTS, max(width, depth), NW), BF16),
            pltpu.VMEM((tokens, width), BF16),
            pltpu.VMEM((tokens, heads), BF16),
            pltpu.VMEM((2, own, width), BF16),
            pltpu.VMEM((rows, ff), BF16),
            pltpu.VMEM((all_tiles, rows, TW), F32),
            pltpu.VMEM((all_tiles, 2, own, HW), F32),
            pltpu.VMEM((all_tiles, 2, own, TW), F32),
            pltpu.VMEM((all_tiles, rows, TW), BF16),
            pltpu.SemaphoreType.DMA((SLOTS,)),
            pltpu.SemaphoreType.DMA((4,)),
            pltpu.SemaphoreType.DMA((all_tiles,)),
            pltpu.SemaphoreType.DMA((all_tiles,)),
            pltpu.SemaphoreType.DMA((all_tiles,)),
            pltpu.SemaphoreType.DMA((all_tiles,)),
            pltpu.SemaphoreType.DMA((4,)),
            pltpu.SemaphoreType.DMA,
        ],
        compiler_params=pltpu.CompilerParams(collective_id=0, has_side_effects=True, vmem_limit_bytes=VMEM_LIMIT),
        cost_estimate=pl.CostEstimate(flops=flops, bytes_accessed=6 * width * ff * 2, transcendentals=tokens * ff),
    )(normed, x_in, attn_tok, w_o, w_gate, w_up, w_down)


def solution(mesh):
    sp_size = mesh.shape["sp"]
    tp_size = mesh.shape["tp"]
    row_spec = P(("rep", "sp"), None)
    cache_spec = P("rep", ("tp", "sp"), None)

    def layer_block(x_in, positions, norm_gain, w_q, w_k, w_v, w_o, w_gate, w_up, w_down):
        tok_local = x_in.shape[0]
        heads_tp = w_q.shape[1] // HEAD_DIM
        kv_tp = w_k.shape[1] // HEAD_DIM
        kv_repeat = sp_size // kv_tp
        normed = rms_norm(x_in, norm_gain)
        cos_tab, sin_tab = rope_tables(positions)
        q_rot = rotate(jnp.dot(normed, w_q, preferred_element_type=F32).reshape(tok_local, heads_tp, HEAD_DIM), cos_tab, sin_tab)
        k_rot = rotate(jnp.dot(normed, w_k, preferred_element_type=F32).reshape(tok_local, kv_tp, HEAD_DIM), cos_tab, sin_tab)
        v_val = jnp.dot(normed, w_v, preferred_element_type=F32).astype(BF16).reshape(tok_local, kv_tp, HEAD_DIM)
        q_send = q_rot.reshape(tok_local, sp_size, 1, HEAD_DIM)
        k_send = jnp.repeat(k_rot, kv_repeat, axis=1).reshape(tok_local, sp_size, 1, HEAD_DIM)
        v_send = jnp.repeat(v_val, kv_repeat, axis=1).reshape(tok_local, sp_size, 1, HEAD_DIM)
        send_buf = jnp.concatenate([q_send, k_send, v_send], axis=2)
        recv_buf = lax.all_to_all(send_buf, "sp", 1, 0, tiled=True)
        recv_buf = recv_buf.reshape(tok_local * sp_size, 3, HEAD_DIM)
        q_all = recv_buf[:, 0]
        k_all = recv_buf[:, 1]
        v_all = recv_buf[:, 2]
        attn_head = attention(q_all, k_all, v_all)
        attn_tok = lax.all_to_all(attn_head.reshape(sp_size * tok_local, 1, HEAD_DIM), "sp", 0, 1, tiled=True).reshape(tok_local, heads_tp * HEAD_DIM)
        y_out = ring_mlp(tp_size, normed, x_in, attn_tok, w_o, w_gate, w_up, w_down)
        return y_out, k_all[:, None, :], v_all[:, None, :]

    return jax.shard_map(
        layer_block,
        mesh=mesh,
        in_specs=(row_spec, P(("rep", "sp")), P(None), P(None, "tp"), P(None, "tp"), P(None, "tp"), P("tp", None), P(None, "tp"), P(None, "tp"), P("tp", None)),
        out_specs=(row_spec, cache_spec, cache_spec),
        check_vma=False,
    )
```

time: 759 us -> 358 us (0.47)
  waiting for transfers between devices: 360 us -> 0 us
  matrix products: 276 us -> 12.9 us
  Pallas kernels: 0 us -> 251 us
  blocking collectives: 0 us -> 61.8 us
  other arithmetic: 37.6 us -> 13.4 us
  loops' own time: 21.3 us -> 0 us
  local copies, waits for them, and re-layouts: 34.6 us -> 15.4 us
  between operations: 14.2 us -> 0.94 us
  starting transfers between devices: 11.5 us -> 0 us
    psum x1 -> x0, waiting for transfers between devices: 360 us -> none  [layer_block(): mlp_sum = lax.psum(gated_mlp(normed, w_gate, w_up, w_down), 'tp')]
    dot_general x71 -> x3, matrix products: 276 us -> 12.9 us  [the longest x1 9.83 us: layer_block(): jnp.dot(normed, w_q, preferred_element_type=F32)]
    pallas_call x0 -> x2, Pallas kernels: none -> 251 us  [the longest x1 223 us: ring_mlp(): pl.pallas_call(functools.partial(ring_kernel, ring), out_shape=jax.ShapeD...]
    all_to_all x0 -> x2, blocking collectives: none -> 61.8 us  [the longest x1 43.2 us: layer_block(): recv_buf = lax.all_to_all(send_buf, 'sp', 1, 0, tiled=True)]
    another operation x1 -> x0, loops' own time: 21.3 us -> none  [causal_attention(): attn_tiles = lax.map(attend_tile, jnp.arange(tokens_q // tile_rows))]
    dynamic_slice x32 -> x0, local copies, waits for them, and re-layouts: 18.6 us -> none  [causal_attention(): attn_tiles = lax.map(attend_tile, jnp.arange(tokens_q // tile_rows))]
    reduce_sum x32 -> x0, other arithmetic: 14.3 us -> none  [attend_tile(): weight_total = jnp.sum(weights, axis=-1)]
    all_to_all x2 -> x0, starting transfers between devices: 11.5 us -> none  [the longest x1 6.42 us: layer_block(): recv_buf = lax.all_to_all(send_buf, 'sp', 1, 0, tiled=True)]
  transfers between devices with their start and end apart: 3 -> 0, of which waited for: 1 -> 0; matrix products, arithmetic and copies ran while one was open for 22% -> 0% of each run, Pallas kernels for 0% -> 0%
where the time goes in v1:
time: 358 us; the launch traced here: 356 us
  Pallas kernels  251 us (70%)
  blocking collectives  61.8 us (17%)
  local copies, waits for them, and re-layouts  15.4 us (4%)
  other arithmetic  13.4 us (4%)
  matrix products  12.9 us (4%)
    pallas_call x1, Pallas kernels, ring_mlp(): pl.pallas_call(functools.partial(ring_kernel, ring), out_shape=jax.ShapeD...  223 us
    all_to_all x1, blocking collectives, layer_block(): recv_buf = lax.all_to_all(send_buf, 'sp', 1, 0, tiled=True)  43.2 us
    pallas_call x1, Pallas kernels, attention(): pl.pallas_call(functools.partial(attention_kernel, rows=rows), grid=(tile...  28.8 us
    all_to_all x1, blocking collectives, layer_block(): lax.all_to_all(attn_head.reshape(sp_size * tok_local, 1, HEAD_DIM), 'sp',...  18.6 us
    unnamed x24, local copies, waits for them, and re-layouts  10.8 us
    dot_general x1, matrix products, layer_block(): jnp.dot(normed, w_q, preferred_element_type=F32)  9.83 us

profile of v1, /device:TPU:97, one launch (start us, length us, event | category | flops | bytes accessed | tf_op | source)
XLA Modules:
  0.0 355.8 jit_solution(7816617661605240402)
XLA Ops:
  0.7 3.6 %fusion = f32[512]{0:T(512)S(1)} fusion(bf16[512,5120]{1,0:T(8,128)(2,1)} %x_hbm.1), kind=kLoop, calls=%fused_computation.2 | loop fusion | flops 7863808 | bytes 5244928 | tf_op jit(solution)/shard_map/reduce_sum | solution.py:29
  4.3 0.5 multiply_cosine_fusion
  5.1 4.6 %fusion.2.u_hbm = bf16[512,5120]{1,0:T(8,128)(2,1)S(1)} fusion(bf16[512,5120]{1,0:T(8,128)(2,1)} %x_hbm.1, f32[5120]{0:T(1024)S(1)} %copy-done.3, f32[512]{0:T(512)S(1)} %add_rsqrt_fusion), kind=kLoop, calls=%fused_computation.4 | loop fusion | flops 10485760 | bytes 10508288 | tf_op jit(solution)/shard_map/convert_element_type | solution.py:30
  9.7 1.6 fusion.7
  11.3 0.8 copy-done.2
  12.3 9.8 %convolution_bitcast_fusion = f32[64,8,8,128]{3,1,2,0:T(8,128)S(1)} fusion(bf16[512,5120]{1,0:T(8,128)(2,1)} %copy-done.2, bf16[5120,1024]{1,0:T(8,128)(2,1)} %param.13), kind=kOutput, calls=%fused_computation.8 | convolution fusion | flops 5368709120 | bytes 17825792 | tf_op jit(solution)/shard_map/dot_general | solution.py:360
  22.2 0.5 copy.53
  22.7 2.0 fusion.6
  24.7 1.4 copy-done.6
  26.3 1.6 convolution_convert_fusion
  28.0 2.4 fusion.3
  30.7 0.7 pad_maximum_fusion
  31.5 43.2 %all_to_all.30 = bf16[512,8,3,128]{3,0,2,1:T(8,128)(2,1)S(1)} all-to-all(bf16[512,8,3,128]{3,0,2,1:T(8,128)(2,1)S(1)} %pad_maximum_fusion), channel_id=1, replica_groups=mesh['rep'=1,'tp'=4,'sp'=8] {'sp'}, dimensions={1} | all-to-all | bytes 6291456 | tf_op jit(solution)/shard_map/all_to_all | solution.py:367
  74.7 0.3 copy.47
  75.3 28.8 %shard_map.121 = bf16[4096,128]{1,0:T(8,128)(2,1)S(1)} custom-call(bf16[4096,128]{1,0:T(8,128)(2,1)S(1)} %get-tuple-element.7.q_ref, bf16[4096,128]{1,0:T(8,128)(2,1)S(1)} %bitcast.39, bf16[4096,128]{1,0:T(8,128)(2,1)S(1)} %bitcast.38), custom_call_target="tpu_custom_call" | custom-call | flops 4294967296 | bytes 4194304 | tf_op jit(solution)/shard_map/pallas_call | solution.py:85
  104.1 0.5 broadcast.48
  104.6 1.4 reduce
  106.1 0.3 reshape.124
  106.4 18.6 %all_to_all.31 = bf16[8,2,32768]{2,1,0:T(2,128)(2,1)S(1)} all-to-all(bf16[8,2,32768]{2,1,0:T(2,128)(2,1)S(1)} %reshape.124), channel_id=1, replica_groups=mesh['rep'=1,'tp'=4,'sp'=8] {'sp'}, dimensions={0} | all-to-all | bytes 2097152 | tf_op jit(solution)/shard_map/all_to_all | solution.py:373
  124.9 1.0 reshape.125
  126.1 0.7 copy.49
  126.8 1.3 copy.68
  128.1 222.5 %shard_map.122 = bf16[512,5120]{1,0:T(8,128)(2,1)} custom-call(bf16[512,5120]{1,0:T(8,128)(2,1)} %copy-done.2, bf16[512,5120]{1,0:T(8,128)(2,1)} %x_hbm.1, bf16[512,1024]{1,0:T(8,128)(2,1)} %bitcast.49, bf16[1024,5120]{1,0:T(8,128)(2,1)} %wo_hbm.1, bf16[5120,8192]{1,0:T(8,128)(2,1)} %wg_hbm.1, bf16[5120,8192]{1,0:T(8,128)(2,1)} %wu_hbm.1, ...), custom_call_target="tpu_custom_call" | custom-call | flops 134217728000 | bytes 503316480 | tf_op jit(solution)/shard_map/pallas_call | solution.py:318
  350.6 5.2 %copy.71 = bf16[512,5120]{1,0:T(8,128)(2,1)} copy(bf16[512,5120]{1,0:T(8,128)(2,1)} %shard_map.122) | data formatting | bytes 10485760
  (30 shorter events, 1.6 us)
Async XLA Ops:
  0.6 3.6 %copy-start.4 = (s32[512]{0:T(512)S(1)}, s32[512]{0:T(512)}, u32[]{:S(2)}) copy-start(s32[512]{0:T(512)} %param.11) | copy-start | bytes 6148
  0.6 4.4 %copy-start.3 = (f32[5120]{0:T(1024)S(1)}, f32[5120]{0:T(1024)}, u32[]{:S(2)}) copy-start(f32[5120]{0:T(1024)} %param.12) | copy-start | bytes 61444
  5.1 4.6 %copy-start.5 = (bf16[5120,256]{1,0:T(8,128)(2,1)S(1)}, bf16[5120,256]{1,0:T(8,128)(2,1)}, u32[]{:S(2)}) copy-start(bf16[5120,256]{1,0:T(8,128)(2,1)} %param.14) | copy-start | bytes 7864324
  9.7 2.4 copy-start.2
  22.2 2.5 slice-start
  22.7 3.4 copy-start.6
  22.7 3.6 %slice-start.1 = ((s8[5242880]{0:T(1024)(128)(4,1)}), s8[1048576]{0:T(1024)(128)(4,1)S(1)}, s32[]{:S(2)}) async-start(s8[5242880]{0:T(1024)(128)(4,1)} %bitcast.43), calls=%async_computation.3 | async-start | bytes 2097152
  75.2 28.9 %copy-start = (bf16[4096,1,128]{2,0,1:T(8,128)(2,1)}, bf16[4096,1,128]{2,0,1:T(8,128)(2,1)S(1)}, u32[]{:S(2)}) copy-start(bf16[4096,1,128]{2,0,1:T(8,128)(2,1)S(1)} %get-tuple-element.19) | copy-start | bytes 3145732
  75.2 28.9 %copy-start.1 = (bf16[4096,1,128]{2,0,1:T(8,128)(2,1)}, bf16[4096,1,128]{2,0,1:T(8,128)(2,1)S(1)}, u32[]{:S(2)}) copy-start(bf16[4096,1,128]{2,0,1:T(8,128)(2,1)S(1)} %get-tuple-element.18) | copy-start | bytes 3145732
